TPU v7x, 32 devices: a whole 2x2x4 slice. The times are simulated.
32 devices in a mesh: gx: 8 (over z, x), gy: 4 (over y, core).
Axes of the slice: x: 2, y: 2, z: 4, core: 2. Of those that a mesh axis runs over, the one named last changes fastest.
Arguments:
- velocity: float32 [3, 64, 256, 256], P(None, 'gx', 'gy'), may hold values from -10 to 10
Outputs:
- coefficient: float32 [256], P('gy')
- viscosity: float32 [64, 256, 256], P('gx', 'gy')
All inputs are finite; a program needn't handle non-finite values.
Results may differ from a plain program's by a relative error of at most 0.00002.
Values sent between devices are 32-bit elements; how exact they have to be, the bound alone decides.
No kernel may reach another device: no remote copies, remote signals or barrier semaphores. Data moves between devices by JAX's collectives and lax.ppermute only.
A program may use at most 64 MiB of HBM per device.

v0:
```python
import jax
import jax.numpy as jnp
from jax import lax
from jax.sharding import PartitionSpec as P

step_stream = 2.0
step_wall = 0.5
step_span = 1.0
clip_high = 0.1
weights = (1.0, 1.0, 1.0, 2.0, 2.0, 2.0)
index_pairs = ((0, 0), (1, 1), (2, 2), (0, 1), (0, 2), (1, 2))


def padded_2(cells, sides, width, closed):
    for axis, dim in sides:
        count = lax.axis_size(axis)
        ends = count if closed else count - 1
        head = lax.slice_in_dim(cells, 0, width, axis=dim)
        tail = lax.slice_in_dim(cells, cells.shape[dim] - width, cells.shape[dim], axis=dim)
        cells = jnp.concatenate(
            [
                lax.ppermute(tail, axis, [(i, (i + 1) % count) for i in range(ends)]),
                cells,
                lax.ppermute(head, axis, [((i + 1) % count, i) for i in range(ends)]),
            ],
            axis=dim,
        )
    return cells


def strain_inner(padded):
    grad_stream = (padded[:, 2:, 1:-1] - padded[:, :-2, 1:-1]) * (0.5 / step_stream)
    grad_wall = (padded[:, 1:-1, 2:] - padded[:, 1:-1, :-2]) * (0.5 / step_wall)
    centre = padded[:, 1:-1, 1:-1]
    grad_span = (jnp.roll(centre, -1, 3) - jnp.roll(centre, 1, 3)) * (0.5 / step_span)
    gradients = (grad_stream, grad_wall, grad_span)
    return jnp.stack(
        [
            0.5 * (gradients[second][first] + gradients[first][second])
            for first, second in index_pairs
        ]
    )


def weight_column():
    return jnp.asarray(weights, jnp.float32).reshape(6, 1, 1, 1)


def magnitude(strain):
    return jnp.sqrt(2.0 * jnp.sum(weight_column() * strain * strain, axis=0))


def test_filter(field):
    smoothed = 0.25 * field[:, :-2] + 0.5 * field[:, 1:-1] + 0.25 * field[:, 2:]
    return 0.25 * jnp.roll(smoothed, 1, 3) + 0.5 * smoothed + 0.25 * jnp.roll(smoothed, -1, 3)


def plane_sums(velocity_pad, stress_pad, filtered_pad):
    strain_hat = strain_inner(filtered_pad)
    magnitude_hat = magnitude(strain_hat)
    row_values = velocity_pad[:, :, 1:-1]
    products = jnp.stack([row_values[first] * row_values[second] for first, second in index_pairs])
    product_hat = test_filter(products)
    centre = filtered_pad[:, 1:-1, 1:-1]
    leonard = product_hat - jnp.stack(
        [centre[first] * centre[second] for first, second in index_pairs]
    )
    trace_third = (leonard[0] + leonard[1] + leonard[2]) / 3.0
    leonard = jnp.concatenate([leonard[:3] - trace_third[None], leonard[3:]])
    model_tensor = 2.0 * (test_filter(stress_pad) - 4.0 * magnitude_hat[None] * strain_hat)
    numerator = jnp.sum(weight_column() * leonard * model_tensor, axis=(0, 1, 3))
    denominator = jnp.sum(weight_column() * model_tensor * model_tensor, axis=(0, 1, 3))
    return (numerator, denominator)


def local(velocity):
    wall_count = lax.axis_size("gy")
    wall_index = lax.axis_index("gy")
    padded = padded_2(velocity, (("gx", 1), ("gy", 2)), 2, True)
    row_ids = jnp.arange(padded.shape[2])
    interior = padded.shape[2] - 2 * 2
    low_wall = jnp.logical_and(wall_index == 0, row_ids < 2)
    high_wall = jnp.logical_and(wall_index == wall_count - 1, row_ids >= interior + 2)
    inside = jnp.logical_not(jnp.logical_or(low_wall, high_wall))
    wide_pad = jnp.where(inside[None, None, :, None], padded, 0.0)
    velocity_pad = wide_pad[:, 1:-1, 1:-1]
    strain_wide = strain_inner(wide_pad)
    strength_wide = magnitude(strain_wide)
    stress_pad = (strength_wide[None] * strain_wide)[:, :, 1:-1]
    strength = strength_wide[1:-1, 1:-1]
    filtered_pad = test_filter(wide_pad[:, :, 1:-1])
    numerator, denominator = plane_sums(velocity_pad, stress_pad, filtered_pad)
    numerator, denominator = lax.psum((numerator, denominator), "gx")
    raw_profile = jnp.clip(numerator / denominator, 0.0, clip_high)
    rim_values = padded_2(raw_profile, (("gy", 0),), 1, False)
    bottom = jnp.where(wall_index == 0, raw_profile[0], rim_values[0])
    top_edge = jnp.where(wall_index == wall_count - 1, raw_profile[-1], rim_values[-1])
    below_values = jnp.concatenate([bottom[None], raw_profile[:-1]])
    above_values = jnp.concatenate([raw_profile[1:], top_edge[None]])
    smooth = 0.25 * below_values + 0.5 * raw_profile + 0.25 * above_values
    return (smooth, smooth[None, :, None] * strength)


def solution(mesh):
    in_specs = (P(None, "gx", "gy", None),)
    out_specs = (P("gy"), P("gx", "gy", None))
    return jax.shard_map(local, mesh=mesh, in_specs=in_specs, out_specs=out_specs, check_vma=False)
```

profile of v0, /device:TPU:0, one launch (start us, length us, event | category | flops | bytes accessed | tf_op | source)
XLA Modules:
  0.0 102.6 jit_solution(11081968702126409254)
XLA Ops:
  0.6 1.3 %fusion.60 = (f32[3,2,64,256]{3,2,1,0:T(8,128)S(1)}, f32[3,2,64,256]{3,2,1,0:T(8,128)S(1)}) fusion(f32[3,8,64,256]{3,2,1,0:T(8,128)} %param.5), kind=kLoop, calls=%fused_computation.122 | loop fusion | bytes 1572864 | tf_op jit(solution)/shard_map/slice | solution.py:18
  2.0 3.0 %collective-permute-start = (f32[3,2,64,256]{3,2,1,0:T(8,128)S(1)}, f32[3,2,64,256]{3,2,1,0:T(8,128)S(1)}, u32[]{:S(2)}, u32[]{:S(2)}) collective-permute-start(f32[3,2,64,256]{3,2,1,0:T(8,128)S(1)} %get-tuple-element.36), channel_id=1, source_target_pairs={{0,4},{4,8},{8,12},{12,16},{16,20},{20,24},{24,28},{28,0},{1,5},{5... | collective-permute-start | bytes 1179656 | tf_op jit(solution)/shard_map/ppermute | solution.py:22
  5.0 3.1 %collective-permute-start.1 = (f32[3,2,64,256]{3,2,1,0:T(8,128)S(1)}, f32[3,2,64,256]{3,2,1,0:T(8,128)S(1)}, u32[]{:S(2)}, u32[]{:S(2)}) collective-permute-start(f32[3,2,64,256]{3,2,1,0:T(8,128)S(1)} %get-tuple-element.35), channel_id=1, source_target_pairs={{4,0},{8,4},{12,8},{16,12},{20,16},{24,20},{28,24},{0,28},{5,1},{9... | collective-permute-start | bytes 1179656 | tf_op jit(solution)/shard_map/ppermute | solution.py:24
  8.1 13.7 %collective-permute-done = f32[3,2,64,256]{3,2,1,0:T(8,128)S(1)} collective-permute-done((f32[3,2,64,256]{3,2,1,0:T(8,128)S(1)}, f32[3,2,64,256]{3,2,1,0:T(8,128)S(1)}, u32[]{:S(2)}, u32[]{:S(2)}) %collective-permute-start) | collective-permute-done | bytes 393248 | tf_op jit(solution)/shard_map/ppermute | solution.py:22
  22.0 2.0 %collective-permute-done.1 = f32[3,2,64,256]{3,2,1,0:T(8,128)S(1)} collective-permute-done((f32[3,2,64,256]{3,2,1,0:T(8,128)S(1)}, f32[3,2,64,256]{3,2,1,0:T(8,128)S(1)}, u32[]{:S(2)}, u32[]{:S(2)}) %collective-permute-start.1) | collective-permute-done | bytes 393248 | tf_op jit(solution)/shard_map/ppermute | solution.py:24
  24.6 1.5 %collective-permute-done.3 = f32[3,12,2,256]{3,2,1,0:T(2,128)S(1)} collective-permute-done((f32[3,12,2,256]{3,2,1,0:T(2,128)S(1)}, f32[3,12,2,256]{3,2,1,0:T(2,128)S(1)}, u32[]{:S(2)}, u32[]{:S(2)}) %collective-permute-start.3) | collective-permute-done | bytes 73760 | tf_op jit(solution)/shard_map/ppermute | solution.py:24
  26.1 2.6 %collective-permute-done.2 = f32[3,12,2,256]{3,2,1,0:T(2,128)S(1)} collective-permute-done((f32[3,12,2,256]{3,2,1,0:T(2,128)S(1)}, f32[3,12,2,256]{3,2,1,0:T(2,128)S(1)}, u32[]{:S(2)}, u32[]{:S(2)}) %collective-permute-start.2) | collective-permute-done | bytes 73760 | tf_op jit(solution)/shard_map/ppermute | solution.py:22
  30.7 1.4 %fusion.59 = (f32[3,10,66,1]{3,2,1,0:T(8,128)S(1)}, f32[3,10,66,1]{3,2,1,0:T(8,128)}) fusion(f32[3,10,66,256]{3,2,1,0:T(8,128)S(1)} %get-tuple-element.16), kind=kLoop, calls=%fused_computation.121 | loop fusion | bytes 31680 | tf_op jit(solution)/shard_map/jit(_roll_static)/slice | solution.py:55
  33.2 1.2 %fusion.49 = (f32[6,8,64,255]{3,2,1,0:T(8,128)S(1)}, f32[6,8,64,255]{3,2,1,0:T(8,128)S(1)}) fusion(f32[6,8,64,256]{3,2,1,0:T(8,128)S(1)} %fusion.4), kind=kLoop, calls=%fused_computation.111 | loop fusion | bytes 12533760 | tf_op jit(solution)/shard_map/jit(_roll_static)/slice | solution.py:55
  34.4 2.3 %fusion.50 = (f32[6,8,64,1]{3,2,1,0:T(8,128)}, f32[6,8,64,1]{3,2,1,0:T(8,128)}) fusion(f32[6,8,64,256]{3,2,1,0:T(8,128)S(1)} %fusion.4), kind=kLoop, calls=%fused_computation.112 | loop fusion | bytes 49152 | tf_op jit(solution)/shard_map/jit(_roll_static)/slice | solution.py:55
  36.7 2.6 %fusion.17 = f32[3,10,66,256]{3,2,1,0:T(8,128)S(1)} fusion(f32[3,10,66,255]{3,2,1,0:T(8,128)S(1)} %get-tuple-element.32, f32[3,10,66,1]{3,2,1,0:T(8,128)} %get-tuple-element.34, f32[3,10,66,1]{3,2,1,0:T(8,128)S(1)} %get-tuple-element.33, f32[3,10,66,255]{3,2,1,0:T(8,128)S(1)} %get-tuple-element.31, f32[3,10,66,256]{3,2,1,0:T(8,128)S(1)} %get-tuple-element.16), kind=kLoop, calls=%fused_computation.35 | loop fusion | flops 3548160 | bytes 8110080 | tf_op jit(solution)/shard_map/add | solution.py:55
  39.2 0.9 multiply_dynamic-update-slice_fusion.11
  40.1 2.2 %fusion.57 = (f32[3,8,64,255]{3,2,1,0:T(8,128)}, f32[3,8,64,255]{3,2,1,0:T(8,128)}) fusion(f32[3,10,66,256]{3,2,1,0:T(8,128)S(1)} %fusion.17), kind=kLoop, calls=%fused_computation.119 | loop fusion | bytes 6266880 | tf_op jit(solution)/shard_map/jit(_roll_static)/slice | solution.py:35
  42.3 1.4 %fusion.56 = (f32[3,8,64,1]{3,2,1,0:T(8,128)}, f32[3,8,64,1]{3,2,1,0:T(8,128)}) fusion(f32[3,10,66,256]{3,2,1,0:T(8,128)S(1)} %fusion.17), kind=kLoop, calls=%fused_computation.118 | loop fusion | bytes 24576 | tf_op jit(solution)/shard_map/jit(_roll_static)/slice | solution.py:35
  45.0 1.0 fusion.18
  49.1 1.8 %fusion.52 = (f32[6,8,64,1]{3,2,1,0:T(8,128)S(1)}, f32[6,8,64,1]{3,2,1,0:T(8,128)}) fusion(f32[6,8,64,256]{3,2,1,0:T(8,128)S(1)} %fusion.2), kind=kLoop, calls=%fused_computation.114 | loop fusion | bytes 49152 | tf_op jit(solution)/shard_map/jit(_roll_static)/slice | solution.py:55
  50.9 3.0 %fusion.51 = (f32[6,8,64,255]{3,2,1,0:T(8,128)S(1)}, f32[6,8,64,255]{3,2,1,0:T(8,128)}) fusion(f32[6,8,64,256]{3,2,1,0:T(8,128)S(1)} %fusion.2), kind=kLoop, calls=%fused_computation.113 | loop fusion | bytes 12533760 | tf_op jit(solution)/shard_map/jit(_roll_static)/slice | solution.py:55
  53.9 0.9 multiply_dynamic-update-slice_fusion.10
  54.8 0.9 multiply_dynamic-update-slice_fusion.9
  55.6 0.9 multiply_dynamic-update-slice_fusion.8
  56.5 0.9 multiply_dynamic-update-slice_fusion.7
  57.4 0.9 multiply_dynamic-update-slice_fusion.6
  58.3 3.8 %fusion.8 = f32[6,8,64,256]{3,2,1,0:T(8,128)S(1)} fusion(f32[6,8,64,256]{3,2,1,0:T(8,128)} %multiply_dynamic-update-slice_fusion.6, f32[6,8,64,255]{3,2,1,0:T(8,128)S(1)} %get-tuple-element.9, f32[6,8,64,1]{3,2,1,0:T(8,128)S(1)} %copy-done.2, f32[6,8,64,1]{3,2,1,0:T(8,128)S(1)} %copy-done.1, f32[6,8,64,255]{3,2,1,0:T(8,128)S(1)} %get-tuple-element.8, ...), kind=kLoop, calls=%fused_computation.17 | loop fusion | flops 10223616 | bytes 22020096 | tf_op jit(solution)/shard_map/sub | solution.py:65
  62.6 1.0 copy-done.4
  64.1 2.5 %slice_subtract_fusion.1 = (f32[3,8,64,256]{3,2,1,0:T(8,128)S(1)}, f32[3,8,64,256]{3,2,1,0:T(8,128)S(1)}, f32[3,8,64,256]{3,2,1,0:T(8,128)S(1)}) fusion(f32[3,10,66,256]{3,2,1,0:T(8,128)S(1)} %fusion.17, f32[3,8,64,255]{3,2,1,0:T(8,128)S(1)} %copy-done.4, f32[3,8,64,1]{3,2,1,0:T(8,128)} %get-tuple-element.25, f32[3,8,64,1]{3,2,1,0:T(8,128)} %get-tuple-element.26, ...), kind=kLoop, calls=%fused_computation.41 | loop fusion | flops 2752512 | bytes 14155776 | tf_op jit(solution)/shard_map/sub | solution.py:33
  67.7 1.2 %copy-done = f32[6,8,64,255]{3,2,1,0:T(8,128)S(1)} copy-done((f32[6,8,64,255]{3,2,1,0:T(8,128)S(1)}, f32[6,8,64,255]{3,2,1,0:T(8,128)}, u32[]{:S(2)}) %copy-start) | copy-done | bytes 3133464
  69.3 4.1 %multiply_reduce_fusion = (f32[64]{0:T(128)S(1)}, f32[64]{0:T(128)S(1)}) fusion(f32[6]{0:T(128)S(1)} %copy-done.11, f32[3,8,64,256]{3,2,1,0:T(8,128)S(1)} %get-tuple-element.7, f32[3,8,64,256]{3,2,1,0:T(8,128)S(1)} %get-tuple-element.6, f32[6]{0:T(128)S(1)} %copy-done.9, f32[6,8,64,256]{3,2,1,0:T(8,128)S(1)} %fusion.34, ...), kind=kLoop, calls=%fused_computation.27 | loop fusion | flops 17301376 | bytes 22544944 | tf_op jit(solution)/shard_map/reduce_sum | solution.py:72
  73.4 20.7 %all-reduce = (f32[64]{0:T(128)S(1)}, f32[64]{0:T(128)S(1)}) all-reduce(f32[64]{0:T(128)S(1)} %get-tuple-element.3, f32[64]{0:T(128)S(1)} %get-tuple-element.2), channel_id=1, replica_groups=mesh['gx'=8,'gy'=4] {'gx'}, use_global_device_ids=true, to_apply=%region_3.4 | all-reduce | flops 128 | bytes 1024 | tf_op jit(solution)/shard_map/psum | solution.py:93
  94.8 1.8 %collective-permute-start.4 = (f32[1]{0:T(128)}, f32[1]{0:T(128)}, u32[]{:S(2)}, u32[]{:S(2)}) collective-permute-start(f32[1]{0:T(128)} %get-tuple-element.39), channel_id=1, source_target_pairs={{0,1},{1,2},{2,3},{4,5},{5,6},{6,7},{8,9},{9,10},{10,11},{12,13},{... | collective-permute-start | bytes 20 | tf_op jit(solution)/shard_map/ppermute | solution.py:22
  96.6 1.3 %collective-permute-start.5 = (f32[1]{0:T(128)}, f32[1]{0:T(128)}, u32[]{:S(2)}, u32[]{:S(2)}) collective-permute-start(f32[1]{0:T(128)} %get-tuple-element.40), channel_id=1, source_target_pairs={{1,0},{2,1},{3,2},{5,4},{6,5},{7,6},{9,8},{10,9},{11,10},{13,12},{... | collective-permute-start | bytes 20 | tf_op jit(solution)/shard_map/ppermute | solution.py:24
  99.2 1.2 %collective-permute-done.5 = f32[1]{0:T(128)} collective-permute-done((f32[1]{0:T(128)}, f32[1]{0:T(128)}, u32[]{:S(2)}, u32[]{:S(2)}) %collective-permute-start.5) | collective-permute-done | bytes 36 | tf_op jit(solution)/shard_map/ppermute | solution.py:24
  101.7 0.9 slice_multiply_fusion.7
  (66 shorter events, 11.3 us)
Async XLA Ops:
  0.6 21.2 %copy-start.8 = (f32[3,8,64,256]{3,2,1,0:T(8,128)S(1)}, f32[3,8,64,256]{3,2,1,0:T(8,128)}, u32[]{:S(2)}) copy-start(f32[3,8,64,256]{3,2,1,0:T(8,128)} %param.5) | copy-start | bytes 4718596
  2.0 19.8 %collective-permute-start = (f32[3,2,64,256]{3,2,1,0:T(8,128)S(1)}, f32[3,2,64,256]{3,2,1,0:T(8,128)S(1)}, u32[]{:S(2)}, u32[]{:S(2)}) collective-permute-start(f32[3,2,64,256]{3,2,1,0:T(8,128)S(1)} %get-tuple-element.36), channel_id=1, source_target_pairs={{0,4},{4,8},{8,12},{12,16},{16,20},{20,24},{24,28},{28,0},{1,5},{5... | collective-permute-start | bytes 1179656 | tf_op jit(solution)/shard_map/ppermute | solution.py:22
  5.0 19.0 %collective-permute-start.1 = (f32[3,2,64,256]{3,2,1,0:T(8,128)S(1)}, f32[3,2,64,256]{3,2,1,0:T(8,128)S(1)}, u32[]{:S(2)}, u32[]{:S(2)}) collective-permute-start(f32[3,2,64,256]{3,2,1,0:T(8,128)S(1)} %get-tuple-element.35), channel_id=1, source_target_pairs={{4,0},{8,4},{12,8},{16,12},{20,16},{24,20},{28,24},{0,28},{5,1},{9... | collective-permute-start | bytes 1179656 | tf_op jit(solution)/shard_map/ppermute | solution.py:24
  24.1 2.0 %collective-permute-start.3 = (f32[3,12,2,256]{3,2,1,0:T(2,128)S(1)}, f32[3,12,2,256]{3,2,1,0:T(2,128)S(1)}, u32[]{:S(2)}, u32[]{:S(2)}) collective-permute-start(f32[3,12,2,256]{3,2,1,0:T(2,128)S(1)} %get-tuple-element.24), channel_id=1, source_target_pairs={{1,0},{2,1},{3,2},{0,3},{5,4},{6,5},{7,6},{4,7},{9,8},{10,9},{11,1... | collective-permute-start | bytes 221192 | tf_op jit(solution)/shard_map/ppermute | solution.py:24
  24.1 4.6 %collective-permute-start.2 = (f32[3,12,2,256]{3,2,1,0:T(2,128)S(1)}, f32[3,12,2,256]{3,2,1,0:T(2,128)S(1)}, u32[]{:S(2)}, u32[]{:S(2)}) collective-permute-start(f32[3,12,2,256]{3,2,1,0:T(2,128)S(1)} %get-tuple-element.23), channel_id=1, source_target_pairs={{0,1},{1,2},{2,3},{3,0},{4,5},{5,6},{6,7},{7,4},{8,9},{9,10},{10,1... | collective-permute-start | bytes 221192 | tf_op jit(solution)/shard_map/ppermute | solution.py:22
  46.1 0.7 copy-start.9
  47.5 0.9 copy-start.6
  54.7 3.5 %copy-start.1 = (f32[6,8,64,1]{3,2,1,0:T(8,128)S(1)}, f32[6,8,64,1]{3,2,1,0:T(8,128)}, u32[]{:S(2)}) copy-start(f32[6,8,64,1]{3,2,1,0:T(8,128)} %get-tuple-element.10) | copy-start | bytes 36868
  54.7 3.5 %copy-start.2 = (f32[6,8,64,1]{3,2,1,0:T(8,128)S(1)}, f32[6,8,64,1]{3,2,1,0:T(8,128)}, u32[]{:S(2)}) copy-start(f32[6,8,64,1]{3,2,1,0:T(8,128)} %get-tuple-element.11) | copy-start | bytes 36868
  62.2 1.4 %copy-start.4 = (f32[3,8,64,255]{3,2,1,0:T(8,128)S(1)}, f32[3,8,64,255]{3,2,1,0:T(8,128)}, u32[]{:S(2)}) copy-start(f32[3,8,64,255]{3,2,1,0:T(8,128)} %get-tuple-element.27) | copy-start | bytes 4700164
  62.2 1.9 %copy-start.5 = (f32[3,8,64,255]{3,2,1,0:T(8,128)S(1)}, f32[3,8,64,255]{3,2,1,0:T(8,128)}, u32[]{:S(2)}) copy-start(f32[3,8,64,255]{3,2,1,0:T(8,128)} %get-tuple-element.28) | copy-start | bytes 4700164
  66.9 1.9 %copy-start = (f32[6,8,64,255]{3,2,1,0:T(8,128)S(1)}, f32[6,8,64,255]{3,2,1,0:T(8,128)}, u32[]{:S(2)}) copy-start(f32[6,8,64,255]{3,2,1,0:T(8,128)} %get-tuple-element.13) | copy-start | bytes 9400324
  66.9 2.3 %copy-start.3 = (f32[6,8,64,1]{3,2,1,0:T(8,128)S(1)}, f32[6,8,64,1]{3,2,1,0:T(8,128)}, u32[]{:S(2)}) copy-start(f32[6,8,64,1]{3,2,1,0:T(8,128)} %get-tuple-element.15) | copy-start | bytes 36868
  67.0 2.3 %copy-start.11 = (f32[6]{0:T(128)S(1)}, f32[6]{0:T(128)}, u32[]{:S(2)}) copy-start(f32[6]{0:T(128)} %constant.5) | copy-start | bytes 76
  69.3 32.4 %copy-start.7 = (f32[10,66,256]{2,1,0:T(8,128)S(1)}, f32[10,66,256]{2,1,0:T(8,128)}, u32[]{:S(2)}) copy-start(f32[10,66,256]{2,1,0:T(8,128)} %copy-done.6) | copy-start | bytes 2027524
  94.8 3.1 %collective-permute-start.4 = (f32[1]{0:T(128)}, f32[1]{0:T(128)}, u32[]{:S(2)}, u32[]{:S(2)}) collective-permute-start(f32[1]{0:T(128)} %get-tuple-element.39), channel_id=1, source_target_pairs={{0,1},{1,2},{2,3},{4,5},{5,6},{6,7},{8,9},{9,10},{10,11},{12,13},{... | collective-permute-start | bytes 20 | tf_op jit(solution)/shard_map/ppermute | solution.py:22
  96.6 3.7 %collective-permute-start.5 = (f32[1]{0:T(128)}, f32[1]{0:T(128)}, u32[]{:S(2)}, u32[]{:S(2)}) collective-permute-start(f32[1]{0:T(128)} %get-tuple-element.40), channel_id=1, source_target_pairs={{1,0},{2,1},{3,2},{5,4},{6,5},{7,6},{9,8},{10,9},{11,10},{13,12},{... | collective-permute-start | bytes 20 | tf_op jit(solution)/shard_map/ppermute | solution.py:24
  101.7 0.9 copy-start.10
where the time goes:
time: 105 us; the launch traced here: 103 us
  other arithmetic  26.2 us (25%)
  local copies, waits for them, and re-layouts  21.4 us (20%)
  waiting for transfers between devices  21 us (20%)
  blocking collectives  20.7 us (20%)
  starting transfers between devices  9.78 us (9%)
  between operations  3.61 us (3%)
    psum x1, blocking collectives, local(): numerator, denominator = lax.psum((numerator, denominator), 'gx')  20.7 us
    ppermute x3, waiting for transfers between devices, padded_2(): lax.ppermute(tail, axis, [(i, (i + 1) % count) for i in range(ends)])  16.3 us
    slice x6, local copies, waits for them, and re-layouts, test_filter(): jnp.roll(smoothed, -1, 3)  10.3 us
    unnamed x20, other arithmetic  5.43 us
    ppermute x3, starting transfers between devices, padded_2(): lax.ppermute(tail, axis, [(i, (i + 1) % count) for i in range(ends)])  5.34 us
    slice x4, local copies, waits for them, and re-layouts, strain_inner(): jnp.roll(centre, 1, 3)  4.79 us
    ppermute x3, waiting for transfers between devices, padded_2(): lax.ppermute(head, axis, [((i + 1) % count, i) for i in range(ends)])  4.63 us
    ppermute x3, starting transfers between devices, padded_2(): lax.ppermute(head, axis, [((i + 1) % count, i) for i in range(ends)])  4.44 us
  transfers between devices with their start and end apart: 6, of which 5 were waited for; matrix products, arithmetic and copies ran while one was open for 0% of the time, Pallas kernels for 0%

commit v1 on v0

v1 whole, which is shorter than its diff:
```python
import functools

import jax
import jax.numpy as jnp
from jax import lax
from jax.experimental import pallas as pl
from jax.experimental.pallas import tpu as pltpu
from jax.sharding import PartitionSpec as P

clip_high = 0.1
index_pairs = ((0, 0), (1, 1), (2, 2), (0, 1), (0, 2), (1, 2))
scale_x, scale_y, scale_z = 0.25, 1.0, 0.5
TILE = 8


def tile(k):
    return slice(TILE * k, TILE * k + TILE)


def z_pair(value):
    return pltpu.roll(value, 1, 1), pltpu.roll(value, value.shape[1] - 1, 1)


def z_sum(value):
    low, high = z_pair(value)
    return (low + high) + (value + value)


def x_sum(low, value, high):
    return (low + high) + (value + value)


def y_difference(value, row, k, tiles):
    low, high = pltpu.roll(value, 1, 0), pltpu.roll(value, TILE - 1, 0)
    if k < tiles:
        ids = lax.broadcasted_iota(jnp.int32, value.shape, 0)
        before = TILE * k - 1 if k else TILE * tiles + 1
        after = TILE * k + TILE if k < tiles - 1 else TILE * tiles + 5
        low = jnp.where(ids == 0, row(before), low)
        high = jnp.where(ids == TILE - 1, row(after), high)
    return high - low


def strain_of(dx, dy, dz):
    return (
        dx[0] * scale_x,
        dy[1] * scale_y,
        dz[2] * scale_z,
        dy[0] * (0.5 * scale_y) + dx[1] * (0.5 * scale_x),
        dz[0] * (0.5 * scale_z) + dx[2] * (0.5 * scale_x),
        dz[1] * (0.5 * scale_z) + dy[2] * (0.5 * scale_y),
    )


def weighted(a, b):
    diagonal = a[0] * b[0] + a[1] * b[1] + a[2] * b[2]
    off = a[3] * b[3] + a[4] * b[4] + a[5] * b[5]
    return diagonal + (off + off)


def magnitude(strain):
    square = weighted(strain, strain)
    return jnp.sqrt(square + square)


def filter_row(cells, products, smooth, i, tiles, with_products=True):
    for k in range(tiles + 1):
        centre = [cells[c, i, tile(k)] for c in range(3)]
        pairs = [z_pair(value) for value in centre]
        store_filters(centre, pairs, products, smooth, i, k, with_products)


def store_filters(centre, pairs, products, smooth, i, k, with_products=True):
    for c in range(3):
        smooth[c, i, tile(k)] = (pairs[c][0] + pairs[c][1]) + (centre[c] + centre[c])
    if with_products:
        for n, (a, b) in enumerate(index_pairs):
            middle = centre[a] * centre[b]
            products[n, i, tile(k)] = (
                pairs[a][0] * pairs[b][0] + pairs[a][1] * pairs[b][1]
            ) + (middle + middle)


def stress_row(cells, stress, products, smooth, strength, i, s, tiles, filters=True):
    for k in range(tiles + 1):
        centre = [cells[c, i, tile(k)] for c in range(3)]
        pairs = [z_pair(value) for value in centre]
        dx = [cells[c, i + 1, tile(k)] - cells[c, i - 1, tile(k)] for c in range(3)]
        dy = [
            y_difference(centre[c], lambda r, c=c: cells[c, i, r : r + 1], k, tiles)
            for c in range(3)
        ]
        dz = [high - low for low, high in pairs]
        strain = strain_of(dx, dy, dz)
        size = magnitude(strain)
        if strength is not None and k < tiles:
            strength[s, tile(k)] = size
        for n in range(6):
            stress[n, i, tile(k)] = z_sum(size * strain[n])
        if filters:
            store_filters(centre, pairs, products, smooth, i, k)


def smooth_row(smooth, filtered, i, tiles):
    for k in range(tiles + 1):
        for c in range(3):
            filtered[c, i, tile(k)] = (1.0 / 16.0) * x_sum(
                smooth[c, i - 1, tile(k)], smooth[c, i, tile(k)], smooth[c, i + 1, tile(k)]
            )


def model_row(stress, products, filtered, sums, j, tiles):
    for k in range(tiles + 1):
        centre = [filtered[c, j, tile(k)] for c in range(3)]
        dx = [filtered[c, j + 1, tile(k)] - filtered[c, j - 1, tile(k)] for c in range(3)]
        dy = [
            y_difference(centre[c], lambda r, c=c: filtered[c, j, r : r + 1], k, tiles)
            for c in range(3)
        ]
        dz = []
        for c in range(3):
            low, high = z_pair(centre[c])
            dz.append(high - low)
        strain = strain_of(dx, dy, dz)
        size = 64.0 * magnitude(strain)
        model = [
            x_sum(stress[n, j - 1, tile(k)], stress[n, j, tile(k)], stress[n, j + 1, tile(k)])
            - size * strain[n]
            for n in range(6)
        ]
        leonard = [
            (1.0 / 16.0)
            * x_sum(products[n, j - 1, tile(k)], products[n, j, tile(k)], products[n, j + 1, tile(k)])
            - centre[a] * centre[b]
            for n, (a, b) in enumerate(index_pairs)
        ]
        third = (leonard[0] + leonard[1] + leonard[2]) * (1.0 / 3.0)
        leonard = [value - third for value in leonard[:3]] + leonard[3:]
        sums[0, tile(k)] += weighted(leonard, model)
        sums[1, tile(k)] += weighted(model, model)


def loop(start, stop, body):
    def step(i, carry):
        body(i)
        return carry

    lax.fori_loop(start, stop, step, 0)


def edge_tiles(cells, low, high, i, rows):
    first, last = cells[:, i, :1], cells[:, i, rows - 1 : rows]
    zero = jnp.zeros_like(first)
    cells[:, i, rows:] = jnp.concatenate([low, first, zero, last, high, zero], axis=1)


def copies(pairs, sems, base=0):
    return [pltpu.make_async_copy(a, b, sems.at[base + n]) for n, (a, b) in enumerate(pairs)]


def start(work):
    for copy in work:
        copy.start()


def wait(work):
    for copy in work:
        copy.wait()


def kept_rows(own):
    return (
        ((3, 2), (own - 1, 2)),
        ((2, 3), (own - 1, 3)),
        ((2, 2), (own, 2)),
        ((3, 2), (own - 1, 2)),
    )


def kept_pairs(fields, keeps, own):
    out = []
    for field, keep, spans in zip(fields, keeps, kept_rows(own)):
        offset = 0
        for at, count in spans:
            out.append((field.at[:, at : at + count], keep.at[:, offset : offset + count]))
            offset += count
    return out


def inner_kernel(
    v, low, high, sums, strength, stress_keep, products_keep, smooth_keep, filtered_keep,
    stress, products, smooth, filtered, cells, sems,
):
    own, rows = v.shape[1], v.shape[2]
    tiles = rows // TILE
    load = copies([(v, cells.at[:, 2 : own + 2, :rows])], sems)
    start(load)
    sums[...] = jnp.zeros_like(sums)
    wait(load)
    for i in range(own):
        edge_tiles(cells, low[:, i], high[:, i], i + 2, rows)
    loop(0, 2, lambda s: filter_row(cells, products, smooth, 2 + s * (own - 1), tiles))
    loop(
        3,
        own + 1,
        lambda i: stress_row(cells, stress, products, smooth, strength, i, i - 3, tiles),
    )
    loop(3, own + 1, lambda i: smooth_row(smooth, filtered, i, tiles))
    keeps = (stress_keep, products_keep, smooth_keep, filtered_keep)
    save = copies(kept_pairs((stress, products, smooth, filtered), keeps, own), sems, 1)
    start(save[:6])
    loop(4, own, lambda j: model_row(stress, products, filtered, sums, j, tiles))
    start(save[6:])
    wait(save)


def outer_kernel(
    v, left, right, low, high, left_edge, right_edge,
    stress_keep, products_keep, smooth_keep, filtered_keep, sums_in,
    totals, strength,
    stress, products, smooth, filtered, sums, cells, sems,
):
    own, rows = v.shape[1], v.shape[2]
    tiles = rows // TILE
    ends = [
        (left, cells.at[:, 0:2, :rows]),
        (v.at[:, 0:2], cells.at[:, 2:4, :rows]),
        (v.at[:, own - 2 : own], cells.at[:, own : own + 2, :rows]),
        (right, cells.at[:, own + 2 : own + 4, :rows]),
    ]
    load = copies(ends, sems)
    start(load)
    keeps = (stress_keep, products_keep, smooth_keep, filtered_keep)
    kept = kept_pairs((stress, products, smooth, filtered), keeps, own)
    more = copies([(b, a) for a, b in kept], sems, 4)
    start(more)
    sums[...] = sums_in[...]
    wait(load)
    for i in range(2):
        edge_tiles(cells, left_edge[:, i, :2], left_edge[:, i, 2:], i, rows)
        edge_tiles(cells, low[:, i], high[:, i], i + 2, rows)
        edge_tiles(cells, low[:, own - 2 + i], high[:, own - 2 + i], own + i, rows)
        edge_tiles(cells, right_edge[:, i, :2], right_edge[:, i, 2:], own + 2 + i, rows)

    def side(s):
        filter_row(cells, products, smooth, s * (own + 3), tiles, with_products=False)
        stress_row(cells, stress, products, smooth, None, 1 + s * (own + 1), s, tiles)

    loop(0, 2, side)
    loop(
        0,
        2,
        lambda s: stress_row(
            cells, stress, products, smooth, strength, 2 + s * (own - 1), s, tiles, False
        ),
    )
    wait(more)
    loop(0, 4, lambda t: smooth_row(smooth, filtered, 1 + t + (t // 2) * (own - 2), tiles))
    loop(
        0,
        4,
        lambda t: model_row(
            stress, products, filtered, sums, 2 + t + (t // 2) * (own - 4), tiles
        ),
    )
    for n in range(2):
        value = sums[n]
        folded = value[:, : value.shape[1] // 2] + value[:, value.shape[1] // 2 :]
        totals[n : n + 1] = jnp.sum(folded.T, axis=0, keepdims=True)


def shift(count, step, closed):
    pairs = [(i, i + step) for i in range(count)]
    if closed:
        return [(i, j % count) for i, j in pairs]
    return [(i, j) for i, j in pairs if 0 <= j < count]


def vmem(n):
    return [pl.BlockSpec(memory_space=pltpu.VMEM)] * n


def anywhere(n):
    return [pl.BlockSpec(memory_space=pl.ANY)] * n


def sum_over(value, axis):
    count = lax.axis_size(axis)
    if count & (count - 1):
        return lax.psum(value, axis)
    step = 1
    while step < count:
        value = value + lax.ppermute(value, axis, [(i, i ^ step) for i in range(count)])
        step *= 2
    return value


def local(v):
    _, own, rows, span = v.shape
    wall_count = lax.axis_size("gy")
    stream_count = lax.axis_size("gx")
    wall_index = lax.axis_index("gy")
    float_array = functools.partial(jax.ShapeDtypeStruct, dtype=jnp.float32)

    to_next = shift(stream_count, 1, True)
    to_last = shift(stream_count, -1, True)
    left = lax.ppermute(v[:, own - 2 :], "gx", to_next)
    right = lax.ppermute(v[:, :2], "gx", to_last)
    low = lax.ppermute(v[:, :, rows - 2 :], "gy", shift(wall_count, 1, False))
    high = lax.ppermute(v[:, :, :2], "gy", shift(wall_count, -1, False))
    edges = jnp.concatenate([low, high], axis=2)
    left_edge = lax.ppermute(edges[:, own - 2 :], "gx", to_next)
    right_edge = lax.ppermute(edges[:, :2], "gx", to_last)

    tall = rows + TILE
    wide = own + 4
    kept = tuple(
        float_array((fields, sum(count for _, count in spans), tall, span))
        for fields, spans in zip((6, 6, 3, 3), kept_rows(own))
    )
    fields = [pltpu.VMEM((n, wide, tall, span), jnp.float32) for n in (6, 6, 3, 3)]
    cells = pltpu.VMEM((3, wide, tall, span), jnp.float32)
    params = pltpu.CompilerParams(vmem_limit_bytes=30 * 1024 * 1024)
    inner = pl.pallas_call(
        inner_kernel,
        out_shape=(float_array((2, tall, span)), float_array((own - 2, rows, span))) + kept,
        in_specs=anywhere(1) + vmem(2),
        out_specs=tuple(vmem(2) + anywhere(4)),
        scratch_shapes=fields + [cells, pltpu.SemaphoreType.DMA((9,))],
        compiler_params=params,
        cost_estimate=pl.CostEstimate(flops=60_000_000, transcendentals=0, bytes_accessed=6_000_000),
        name="inner",
    )(v, low, high)
    sums, strength_inner = inner[:2]
    totals, strength_outer = pl.pallas_call(
        outer_kernel,
        out_shape=(float_array((2, tall)), float_array((2, rows, span))),
        in_specs=anywhere(3) + vmem(4) + anywhere(4) + vmem(1),
        out_specs=tuple(vmem(2)),
        scratch_shapes=fields
        + [pltpu.VMEM((2, tall, span), jnp.float32), cells, pltpu.SemaphoreType.DMA((12,))],
        compiler_params=params,
        cost_estimate=pl.CostEstimate(flops=40_000_000, transcendentals=0, bytes_accessed=6_000_000),
        name="outer",
    )(v, left, right, low, high, left_edge, right_edge, *inner[2:], sums)

    totals = sum_over(totals, "gx")
    raw = jnp.clip(8.0 * totals[0] / totals[1], 0.0, clip_high)
    inside = raw[:rows]
    bottom = jnp.where(wall_index == 0, raw[:1], raw[rows + 1 : rows + 2])
    top = jnp.where(wall_index == wall_count - 1, raw[rows - 1 : rows], raw[rows + 5 : rows + 6])
    around = jnp.concatenate([bottom, inside, top])
    coefficient = 0.25 * around[:-2] + 0.5 * inside + 0.25 * around[2:]
    strength = jnp.concatenate([strength_outer[:1], strength_inner, strength_outer[1:]])
    return coefficient, coefficient[None, :, None] * strength


def solution(mesh):
    in_specs = (P(None, "gx", "gy", None),)
    out_specs = (P("gy"), P("gx", "gy", None))
    return jax.shard_map(local, mesh=mesh, in_specs=in_specs, out_specs=out_specs, check_vma=False)
```

time: 105 us -> 51.6 us (0.49); the launches traced: 103 us -> 51.4 us
  other arithmetic: 26.2 us -> 1.11 us
  blocking collectives: 20.7 us -> 0 us
  local copies, waits for them, and re-layouts: 21.4 us -> 2.01 us
  Pallas kernels: 0 us -> 16.2 us
  waiting for transfers between devices: 21 us -> 15.1 us
  starting transfers between devices: 9.78 us -> 13.7 us
    psum x1 -> x0, blocking collectives: 20.7 us -> none  [local(): numerator, denominator = lax.psum((numerator, denominator), 'gx')]
    pallas_call x0 -> x2, Pallas kernels: none -> 16.2 us  [the longest x1 8.91 us: local(): pl.pallas_call(inner_kernel, out_shape=(float_array((2, tall, span)), flo...]
    slice x14 -> x5, local copies, waits for them, and re-layouts: 17.2 us -> 2 us  [the longest x1 1.29 us: local(): right = lax.ppermute(v[:, :2], 'gx', to_last)]
    sub x4 -> x0, other arithmetic: 6.82 us -> none  [the longest x1 3.78 us: plane_sums(): product_hat - jnp.stack([centre[first] * centre[second] for first, second...]
    ppermute x6 -> x9, waiting for transfers between devices: 21 us -> 15.1 us  [the longest x3 11.6 us: sum_over(): lax.ppermute(value, axis, [(i, i ^ step) for i in range(count)])]
    unnamed x20 -> x0, other arithmetic: 5.43 us -> none
    reduce_sum x3 -> x0, other arithmetic: 5.14 us -> none  [the longest x1 4.14 us: plane_sums(): jnp.sum(weight_column() * model_tensor * model_tensor, axis=(0, 1, 3))]
    add x5 -> x4, other arithmetic: 4.64 us -> 0.09 us  [the longest x1 0.08 us: local(): coefficient = 0.25 * around[:-2] + 0.5 * inside + 0.25 * around[2:]]
  transfers between devices with their start and end apart: 6 -> 9, of which waited for: 5 -> 4; matrix products, arithmetic and copies ran while one was open for 0% -> 0% of each run, Pallas kernels for 0% -> 17%
where the time goes in v1:
time: 51.6 us; the launch traced here: 51.4 us
  Pallas kernels  16.2 us (31%)
  waiting for transfers between devices  15.1 us (29%)
  starting transfers between devices  13.7 us (27%)
  between operations  3.28 us (6%)
  local copies, waits for them, and re-layouts  2.01 us (4%)
  other arithmetic  1.11 us (2%)
    ppermute x3, waiting for transfers between devices, sum_over(): lax.ppermute(value, axis, [(i, i ^ step) for i in range(count)])  11.6 us
    pallas_call x1, Pallas kernels, local(): pl.pallas_call(inner_kernel, out_shape=(float_array((2, tall, span)), flo...  8.91 us
    pallas_call x1, Pallas kernels, local(): pl.pallas_call(outer_kernel, out_shape=(float_array((2, tall)), float_arr...  7.25 us
    ppermute x1, starting transfers between devices, local(): right_edge = lax.ppermute(edges[:, :2], 'gx', to_last)  4.71 us
    ppermute x1, waiting for transfers between devices, local(): high = lax.ppermute(v[:, :, :2], 'gy', shift(wall_count, -1, False))  3.53 us
    ppermute x1, starting transfers between devices, local(): right = lax.ppermute(v[:, :2], 'gx', to_last)  3.1 us
    ppermute x1, starting transfers between devices, local(): left = lax.ppermute(v[:, own - 2:], 'gx', to_next)  3.02 us
    ppermute x1, starting transfers between devices, local(): low = lax.ppermute(v[:, :, rows - 2:], 'gy', shift(wall_count, 1, False))  1.46 us
  transfers between devices with their start and end apart: 9, of which 4 were waited for; matrix products, arithmetic and copies ran while one was open for 0% of the time, Pallas kernels for 17%

profile of v1, /device:TPU:0, one launch (start us, length us, event | category | flops | bytes accessed | tf_op | source)
XLA Modules:
  0.0 51.4 jit_solution(7647511689736874526)
XLA Ops:
  0.6 0.0 copy-start
  0.6 1.3 %fusion.2 = (f32[3,2,64,256]{3,2,1,0:T(8,128)S(1)}, f32[3,2,64,256]{3,2,1,0:T(8,128)S(1)}) fusion(f32[3,8,64,256]{3,2,1,0:T(8,128)} %v.3), kind=kLoop, calls=%fused_computation.10 | loop fusion | bytes 1572864 | tf_op jit(solution)/shard_map/slice | solution.py:308
  1.9 3.0 %collective-permute-start = (f32[3,2,64,256]{3,2,1,0:T(8,128)S(1)}, f32[3,2,64,256]{3,2,1,0:T(8,128)S(1)}, u32[]{:S(2)}, u32[]{:S(2)}) collective-permute-start(f32[3,2,64,256]{3,2,1,0:T(8,128)S(1)} %get-tuple-element.21), channel_id=1, source_target_pairs={{0,4},{4,8},{8,12},{12,16},{16,20},{20,24},{24,28},{28,0},{1,5},{5... | collective-permute-start | bytes 1179656 | tf_op jit(solution)/shard_map/ppermute | solution.py:307
  5.0 3.1 %collective-permute-start.1 = (f32[3,2,64,256]{3,2,1,0:T(8,128)S(1)}, f32[3,2,64,256]{3,2,1,0:T(8,128)S(1)}, u32[]{:S(2)}, u32[]{:S(2)}) collective-permute-start(f32[3,2,64,256]{3,2,1,0:T(8,128)S(1)} %get-tuple-element.20), channel_id=1, source_target_pairs={{0,28},{4,0},{8,4},{12,8},{16,12},{20,16},{24,20},{28,24},{1,29},{... | collective-permute-start | bytes 1179656 | tf_op jit(solution)/shard_map/ppermute | solution.py:308
  8.1 0.0 copy-done
  8.1 1.5 %collective-permute-start.2 = (f32[3,8,2,256]{3,2,1,0:T(2,128)S(1)}, f32[3,8,2,256]{3,2,1,0:T(2,128)S(1)}, u32[]{:S(2)}, u32[]{:S(2)}) collective-permute-start(f32[3,8,2,256]{3,2,1,0:T(2,128)S(1)} %get-tuple-element.19), channel_id=1, source_target_pairs={{0,1},{1,2},{2,3},{4,5},{5,6},{6,7},{8,9},{9,10},{10,11},{12,13},{... | collective-permute-start | bytes 147464 | tf_op jit(solution)/shard_map/ppermute | solution.py:309
  9.6 1.3 %collective-permute-start.3 = (f32[3,8,2,256]{3,2,1,0:T(2,128)S(1)}, f32[3,8,2,256]{3,2,1,0:T(2,128)S(1)}, u32[]{:S(2)}, u32[]{:S(2)}) collective-permute-start(f32[3,8,2,256]{3,2,1,0:T(2,128)S(1)} %get-tuple-element.18), channel_id=1, source_target_pairs={{1,0},{2,1},{3,2},{5,4},{6,5},{7,6},{9,8},{10,9},{11,10},{13,12},{... | collective-permute-start | bytes 147464 | tf_op jit(solution)/shard_map/ppermute | solution.py:310
  10.9 0.0 collective-permute-done.2.low
  10.9 3.5 %collective-permute-done.3.high = f32[3,8,2,256]{3,2,1,0:T(2,128)S(1)} collective-permute-done((f32[3,8,2,256]{3,2,1,0:T(2,128)S(1)}, f32[3,8,2,256]{3,2,1,0:T(2,128)S(1)}, u32[]{:S(2)}, u32[]{:S(2)}) %collective-permute-start.3) | collective-permute-done | bytes 49184 | tf_op jit(solution)/shard_map/ppermute | solution.py:310
  14.4 0.1 collective-permute-start.4
  14.5 4.7 %collective-permute-start.5 = (f32[3,2,4,256]{3,2,1,0:T(4,128)S(1)}, f32[3,2,4,256]{3,2,1,0:T(4,128)S(1)}, u32[]{:S(2)}, u32[]{:S(2)}) collective-permute-start(f32[3,2,4,256]{3,2,1,0:T(4,128)S(1)} %get-tuple-element.24), channel_id=1, source_target_pairs={{0,28},{4,0},{8,4},{12,8},{16,12},{20,16},{24,20},{28,24},{1,29},{... | collective-permute-start | bytes 73736 | tf_op jit(solution)/shard_map/ppermute | solution.py:313
  19.2 8.9 %inner.1 = (f32[2,72,256]{2,1,0:T(8,128)S(1)}, f32[6,64,256]{2,1,0:T(8,128)S(1)}, f32[6,4,72,256]{3,2,1,0:T(8,128)S(1)}, f32[6,6,72,256]{3,2,1,0:T(8,128)S(1)}, ...) custom-call(f32[3,8,64,256]{3,2,1,0:T(8,128)S(1)} %copy-done, ...), custom_call_target="tpu_custom_call" | custom-call | flops 60000000 | bytes 6000000 | tf_op jit(solution)/shard_map/inner/pallas_call | solution.py:324
  28.1 0.0 collective-permute-done.4.left_edge
  28.1 0.0 collective-permute-done.5.right_edge
  28.1 0.0 collective-permute-done.left
  28.2 0.0 collective-permute-done.1.right
  28.2 7.2 %outer.1 = (f32[2,72]{1,0:T(2,128)S(1)}, f32[2,64,256]{2,1,0:T(8,128)S(1)}) custom-call(f32[3,8,64,256]{3,2,1,0:T(8,128)S(1)} %copy-done, f32[3,2,64,256]{3,2,1,0:T(8,128)S(1)} %collective-permute-done.left, f32[3,2,64,256]{3,2,1,0:T(8,128)S(1)} %collective-permute-done.1.right, f32[3,8,2,256]{3,2,1,0:T(2,128)S(1)} %collective-permute-done.2.low, ...), custom_call_target="tpu_custom_call" | custom-call | flops 40000000 | bytes 6000000 | tf_op jit(solution)/shard_map/outer/pallas_call | solution.py:335
  35.4 0.1 collective-permute-start.6
  35.5 3.6 %collective-permute-done.6 = f32[2,72]{1,0:T(2,128)S(1)} collective-permute-done((f32[2,72]{1,0:T(2,128)S(1)}, f32[2,72]{1,0:T(2,128)S(1)}, u32[]{:S(2)}, u32[]{:S(2)}) %collective-permute-start.6) | collective-permute-done | bytes 608 | tf_op jit(solution)/shard_map/ppermute | solution.py:293
  39.1 0.0 collective-permute-start.7
  39.1 3.6 %collective-permute-done.7 = f32[2,72]{1,0:T(2,128)S(1)} collective-permute-done((f32[2,72]{1,0:T(2,128)S(1)}, f32[2,72]{1,0:T(2,128)S(1)}, u32[]{:S(2)}, u32[]{:S(2)}) %collective-permute-start.7) | collective-permute-done | bytes 608 | tf_op jit(solution)/shard_map/ppermute | solution.py:293
  42.6 0.0 collective-permute-start.8
  42.7 4.5 %collective-permute-done.8 = f32[2,72]{1,0:T(2,128)S(1)} collective-permute-done((f32[2,72]{1,0:T(2,128)S(1)}, f32[2,72]{1,0:T(2,128)S(1)}, u32[]{:S(2)}, u32[]{:S(2)}) %collective-permute-start.8) | collective-permute-done | bytes 608 | tf_op jit(solution)/shard_map/ppermute | solution.py:293
  47.1 0.7 %fusion.4 = (f32[1,1]{1,0:T(1,128)}, f32[1,1]{1,0:T(1,128)}, f32[1,1]{1,0:T(1,128)}, f32[1,1]{1,0:T(1,128)}) fusion(f32[1,72]{1,0:T(1,128)S(1)} %fusion), kind=kLoop, calls=%fused_computation.12 | loop fusion | bytes 32 | tf_op jit(solution)/shard_map/slice | solution.py:350
  50.3 0.1 pad_maximum_fusion.2
  50.4 0.1 multiply_add_fusion
  50.5 0.0 copy-start.1
  50.5 0.9 %maximum_multiply_fusion = f32[8,64,256]{2,1,0:T(8,128)} fusion(f32[1,64,256]{2,1,0:T(8,128)S(1)} %get-tuple-element.23, f32[6,64,256]{2,1,0:T(8,128)S(1)} %get-tuple-element.17, f32[1,64,256]{2,1,0:T(8,128)S(1)} %get-tuple-element.22, f32[64]{0:T(128)S(1)} %multiply_add_fusion), kind=kLoop, calls=%fused_computation | loop fusion | flops 393216 | bytes 1048832 | tf_op jit(solution)/shard_map/mul | solution.py:355
  51.4 0.0 copy-done.1
  (8 shorter events, 0.1 us)
Async XLA Ops:
  0.6 7.4 %copy-start = (f32[3,8,64,256]{3,2,1,0:T(8,128)S(1)}, f32[3,8,64,256]{3,2,1,0:T(8,128)}, u32[]{:S(2)}) copy-start(f32[3,8,64,256]{3,2,1,0:T(8,128)} %v.3) | copy-start | bytes 4718596
  1.9 26.2 %collective-permute-start = (f32[3,2,64,256]{3,2,1,0:T(8,128)S(1)}, f32[3,2,64,256]{3,2,1,0:T(8,128)S(1)}, u32[]{:S(2)}, u32[]{:S(2)}) collective-permute-start(f32[3,2,64,256]{3,2,1,0:T(8,128)S(1)} %get-tuple-element.21), channel_id=1, source_target_pairs={{0,4},{4,8},{8,12},{12,16},{16,20},{20,24},{24,28},{28,0},{1,5},{5... | collective-permute-start | bytes 1179656 | tf_op jit(solution)/shard_map/ppermute | solution.py:307
  5.0 23.2 %collective-permute-start.1 = (f32[3,2,64,256]{3,2,1,0:T(8,128)S(1)}, f32[3,2,64,256]{3,2,1,0:T(8,128)S(1)}, u32[]{:S(2)}, u32[]{:S(2)}) collective-permute-start(f32[3,2,64,256]{3,2,1,0:T(8,128)S(1)} %get-tuple-element.20), channel_id=1, source_target_pairs={{0,28},{4,0},{8,4},{12,8},{16,12},{20,16},{24,20},{28,24},{1,29},{... | collective-permute-start | bytes 1179656 | tf_op jit(solution)/shard_map/ppermute | solution.py:308
  8.1 2.8 %collective-permute-start.2 = (f32[3,8,2,256]{3,2,1,0:T(2,128)S(1)}, f32[3,8,2,256]{3,2,1,0:T(2,128)S(1)}, u32[]{:S(2)}, u32[]{:S(2)}) collective-permute-start(f32[3,8,2,256]{3,2,1,0:T(2,128)S(1)} %get-tuple-element.19), channel_id=1, source_target_pairs={{0,1},{1,2},{2,3},{4,5},{5,6},{6,7},{8,9},{9,10},{10,11},{12,13},{... | collective-permute-start | bytes 147464 | tf_op jit(solution)/shard_map/ppermute | solution.py:309
  9.6 4.8 %collective-permute-start.3 = (f32[3,8,2,256]{3,2,1,0:T(2,128)S(1)}, f32[3,8,2,256]{3,2,1,0:T(2,128)S(1)}, u32[]{:S(2)}, u32[]{:S(2)}) collective-permute-start(f32[3,8,2,256]{3,2,1,0:T(2,128)S(1)} %get-tuple-element.18), channel_id=1, source_target_pairs={{1,0},{2,1},{3,2},{5,4},{6,5},{7,6},{9,8},{10,9},{11,10},{13,12},{... | collective-permute-start | bytes 147464 | tf_op jit(solution)/shard_map/ppermute | solution.py:310
  14.4 13.7 %collective-permute-start.4 = (f32[3,2,4,256]{3,2,1,0:T(4,128)S(1)}, f32[3,2,4,256]{3,2,1,0:T(4,128)S(1)}, u32[]{:S(2)}, u32[]{:S(2)}) collective-permute-start(f32[3,2,4,256]{3,2,1,0:T(4,128)S(1)} %get-tuple-element.25), channel_id=1, source_target_pairs={{0,4},{4,8},{8,12},{12,16},{16,20},{20,24},{24,28},{28,0},{1,5},{5... | collective-permute-start | bytes 73736 | tf_op jit(solution)/shard_map/ppermute | solution.py:312
  14.5 13.6 %collective-permute-start.5 = (f32[3,2,4,256]{3,2,1,0:T(4,128)S(1)}, f32[3,2,4,256]{3,2,1,0:T(4,128)S(1)}, u32[]{:S(2)}, u32[]{:S(2)}) collective-permute-start(f32[3,2,4,256]{3,2,1,0:T(4,128)S(1)} %get-tuple-element.24), channel_id=1, source_target_pairs={{0,28},{4,0},{8,4},{12,8},{16,12},{20,16},{24,20},{28,24},{1,29},{... | collective-permute-start | bytes 73736 | tf_op jit(solution)/shard_map/ppermute | solution.py:313
  35.4 3.6 %collective-permute-start.6 = (f32[2,72]{1,0:T(2,128)S(1)}, f32[2,72]{1,0:T(2,128)S(1)}, u32[]{:S(2)}, u32[]{:S(2)}) collective-permute-start(f32[2,72]{1,0:T(2,128)S(1)} %get-tuple-element.15), channel_id=1, source_target_pairs={{0,4},{4,0},{8,12},{12,8},{16,20},{20,16},{24,28},{28,24},{1,5},{5... | collective-permute-start | bytes 1736 | tf_op jit(solution)/shard_map/ppermute | solution.py:293
  39.1 3.6 %collective-permute-start.7 = (f32[2,72]{1,0:T(2,128)S(1)}, f32[2,72]{1,0:T(2,128)S(1)}, u32[]{:S(2)}, u32[]{:S(2)}) collective-permute-start(f32[2,72]{1,0:T(2,128)S(1)} %add.15), channel_id=1, source_target_pairs={{0,8},{4,12},{8,0},{12,4},{16,24},{20,28},{24,16},{28,20},{1,9},{5... | collective-permute-start | bytes 1736 | tf_op jit(solution)/shard_map/ppermute | solution.py:293
  42.6 4.5 %collective-permute-start.8 = (f32[2,72]{1,0:T(2,128)S(1)}, f32[2,72]{1,0:T(2,128)S(1)}, u32[]{:S(2)}, u32[]{:S(2)}) collective-permute-start(f32[2,72]{1,0:T(2,128)S(1)} %add.16), channel_id=1, source_target_pairs={{0,16},{4,20},{8,24},{12,28},{16,0},{20,4},{24,8},{28,12},{1,17},{... | collective-permute-start | bytes 1736 | tf_op jit(solution)/shard_map/ppermute | solution.py:293
  50.5 0.9 %copy-start.1 = (f32[64]{0:T(128)}, f32[64]{0:T(128)S(1)}, u32[]{:S(2)}) copy-start(f32[64]{0:T(128)S(1)} %multiply_add_fusion) | copy-start | bytes 772

commit v2 on v1

--- a/solution.py
+++ b/solution.py
@@ -6,6 +6,7 @@
 from jax.experimental import pallas as pl
 from jax.experimental.pallas import tpu as pltpu
 from jax.sharding import PartitionSpec as P
+
 
 clip_high = 0.1
 index_pairs = ((0, 0), (1, 1), (2, 2), (0, 1), (0, 2), (1, 2))
@@ -269,6 +270,29 @@
         totals[n : n + 1] = jnp.sum(folded.T, axis=0, keepdims=True)
 
 
+def final_kernel(totals, strength_inner, strength_outer, coefficient, viscosity):
+    own, rows = viscosity.shape[0], viscosity.shape[1]
+    tall = totals.shape[1]
+    wall_index, wall_count = lax.axis_index("gy"), lax.axis_size("gy")
+    raw = jnp.clip(8.0 * totals[0:1] / totals[1:2], 0.0, clip_high)
+    plane = lax.broadcasted_iota(jnp.int32, (rows, tall), 0)
+    entry = lax.broadcasted_iota(jnp.int32, (rows, tall), 1)
+    below = jnp.where(plane == 0, jnp.where(wall_index == 0, 0, rows + 1), plane - 1)
+    last = plane == rows - 1
+    above = jnp.where(last, jnp.where(wall_index == wall_count - 1, rows - 1, rows + 5), plane + 1)
+    spread = jnp.broadcast_to(raw, (rows, tall))
+    parts = [
+        jnp.where(entry == pick, spread * weight, 0.0)
+        for pick, weight in ((below, 0.25), (plane, 0.5), (above, 0.25))
+    ]
+    column = jnp.sum((parts[0] + parts[2]) + parts[1], axis=1, keepdims=True)
+    square = jnp.where(plane[:, :rows] == entry[:, :rows], column, 0.0)
+    coefficient[...] = jnp.sum(square, axis=0, keepdims=True)
+    for i in range(own):
+        source = strength_outer[i // (own - 1)] if i in (0, own - 1) else strength_inner[i - 1]
+        viscosity[i] = column * source
+
+
 def shift(count, step, closed):
     pairs = [(i, i + step) for i in range(count)]
     if closed:
@@ -299,15 +323,14 @@
     _, own, rows, span = v.shape
     wall_count = lax.axis_size("gy")
     stream_count = lax.axis_size("gx")
-    wall_index = lax.axis_index("gy")
     float_array = functools.partial(jax.ShapeDtypeStruct, dtype=jnp.float32)
 
     to_next = shift(stream_count, 1, True)
     to_last = shift(stream_count, -1, True)
+    low = lax.ppermute(v[:, :, rows - 2 :], "gy", shift(wall_count, 1, False))
+    high = lax.ppermute(v[:, :, :2], "gy", shift(wall_count, -1, False))
     left = lax.ppermute(v[:, own - 2 :], "gx", to_next)
     right = lax.ppermute(v[:, :2], "gx", to_last)
-    low = lax.ppermute(v[:, :, rows - 2 :], "gy", shift(wall_count, 1, False))
-    high = lax.ppermute(v[:, :, :2], "gy", shift(wall_count, -1, False))
     edges = jnp.concatenate([low, high], axis=2)
     left_edge = lax.ppermute(edges[:, own - 2 :], "gx", to_next)
     right_edge = lax.ppermute(edges[:, :2], "gx", to_last)
@@ -345,14 +368,15 @@
     )(v, left, right, low, high, left_edge, right_edge, *inner[2:], sums)
 
     totals = sum_over(totals, "gx")
-    raw = jnp.clip(8.0 * totals[0] / totals[1], 0.0, clip_high)
-    inside = raw[:rows]
-    bottom = jnp.where(wall_index == 0, raw[:1], raw[rows + 1 : rows + 2])
-    top = jnp.where(wall_index == wall_count - 1, raw[rows - 1 : rows], raw[rows + 5 : rows + 6])
-    around = jnp.concatenate([bottom, inside, top])
-    coefficient = 0.25 * around[:-2] + 0.5 * inside + 0.25 * around[2:]
-    strength = jnp.concatenate([strength_outer[:1], strength_inner, strength_outer[1:]])
-    return coefficient, coefficient[None, :, None] * strength
+    coefficient, viscosity = pl.pallas_call(
+        final_kernel,
+        out_shape=(float_array((1, rows)), float_array((own, rows, span))),
+        in_specs=vmem(3),
+        out_specs=tuple(vmem(2)),
+        compiler_params=pltpu.CompilerParams(vmem_limit_bytes=8 * 1024 * 1024),
+        name="final",
+    )(totals, strength_inner, strength_outer)
+    return coefficient[0], viscosity
 
 
 def solution(mesh):

time: 51.6 us -> 47.9 us (0.928)
  the two profiles are of different devices: /device:TPU:0 before, /device:TPU:30 now
where the time goes in v2:
time: 47.9 us; the launch traced here: 47.8 us
  Pallas kernels  17.1 us (36%)
  waiting for transfers between devices  14.6 us (30%)
  starting transfers between devices  13.9 us (29%)
  local copies, waits for them, and re-layouts  1.35 us (3%)
  between operations  0.74 us (2%)
    ppermute x3, waiting for transfers between devices, sum_over(): lax.ppermute(value, axis, [(i, i ^ step) for i in range(count)])  11.6 us
    pallas_call x1, Pallas kernels, local(): pl.pallas_call(inner_kernel, out_shape=(float_array((2, tall, span)), flo...  8.91 us
    pallas_call x1, Pallas kernels, local(): pl.pallas_call(outer_kernel, out_shape=(float_array((2, tall)), float_arr...  7.25 us
    ppermute x1, starting transfers between devices, local(): left_edge = lax.ppermute(edges[:, own - 2:], 'gx', to_next)  4.71 us
    ppermute x1, starting transfers between devices, local(): left = lax.ppermute(v[:, own - 2:], 'gx', to_next)  4.19 us
    ppermute x1, waiting for transfers between devices, local(): low = lax.ppermute(v[:, :, rows - 2:], 'gy', shift(wall_count, 1, False))  2.99 us
    ppermute x1, starting transfers between devices, local(): low = lax.ppermute(v[:, :, rows - 2:], 'gy', shift(wall_count, 1, False))  2.4 us
    ppermute x1, starting transfers between devices, local(): high = lax.ppermute(v[:, :, :2], 'gy', shift(wall_count, -1, False))  1.92 us
  transfers between devices with their start and end apart: 9, of which 4 were waited for; matrix products, arithmetic and copies ran while one was open for 0% of the time, Pallas kernels for 19%

profile of v2, /device:TPU:30, one launch (start us, length us, event | category | flops | bytes accessed | tf_op | source)
XLA Modules:
  0.0 47.8 jit_solution(1451580290711075112)
XLA Ops:
  0.6 0.0 copy-start
  0.6 1.3 %fusion.1 = (f32[3,2,64,256]{3,2,1,0:T(8,128)S(1)}, f32[3,2,64,256]{3,2,1,0:T(8,128)S(1)}) fusion(f32[3,8,64,256]{3,2,1,0:T(8,128)} %v.3), kind=kLoop, calls=%fused_computation.3 | loop fusion | bytes 1572864 | tf_op jit(solution)/shard_map/slice | solution.py:333
  2.0 0.6 %collective-permute-start.1 = (f32[3,2,64,256]{3,2,1,0:T(8,128)S(1)}, f32[3,2,64,256]{3,2,1,0:T(8,128)S(1)}, u32[]{:S(2)}, u32[]{:S(2)}) collective-permute-start(f32[3,2,64,256]{3,2,1,0:T(8,128)S(1)} %get-tuple-element.24), channel_id=1, source_target_pairs={{0,28},{4,0},{8,4},{12,8},{16,12},{20,16},{24,20},{28,24},{1,29},{... | collective-permute-start | bytes 1179656 | tf_op jit(solution)/shard_map/ppermute | solution.py:333
  2.5 4.2 %collective-permute-start = (f32[3,2,64,256]{3,2,1,0:T(8,128)S(1)}, f32[3,2,64,256]{3,2,1,0:T(8,128)S(1)}, u32[]{:S(2)}, u32[]{:S(2)}) collective-permute-start(f32[3,2,64,256]{3,2,1,0:T(8,128)S(1)} %get-tuple-element.25), channel_id=1, source_target_pairs={{0,4},{4,8},{8,12},{12,16},{16,20},{20,24},{24,28},{28,0},{1,5},{5... | collective-permute-start | bytes 1179656 | tf_op jit(solution)/shard_map/ppermute | solution.py:332
  6.7 0.0 copy-done
  6.8 1.9 %collective-permute-start.3 = (f32[3,8,2,256]{3,2,1,0:T(2,128)S(1)}, f32[3,8,2,256]{3,2,1,0:T(2,128)S(1)}, u32[]{:S(2)}, u32[]{:S(2)}) collective-permute-start(f32[3,8,2,256]{3,2,1,0:T(2,128)S(1)} %get-tuple-element.22), channel_id=1, source_target_pairs={{1,0},{2,1},{3,2},{5,4},{6,5},{7,6},{9,8},{10,9},{11,10},{13,12},{... | collective-permute-start | bytes 147464 | tf_op jit(solution)/shard_map/ppermute | solution.py:331
  8.7 2.4 %collective-permute-start.2 = (f32[3,8,2,256]{3,2,1,0:T(2,128)S(1)}, f32[3,8,2,256]{3,2,1,0:T(2,128)S(1)}, u32[]{:S(2)}, u32[]{:S(2)}) collective-permute-start(f32[3,8,2,256]{3,2,1,0:T(2,128)S(1)} %get-tuple-element.23), channel_id=1, source_target_pairs={{0,1},{1,2},{2,3},{4,5},{5,6},{6,7},{8,9},{9,10},{10,11},{12,13},{... | collective-permute-start | bytes 147464 | tf_op jit(solution)/shard_map/ppermute | solution.py:330
  11.1 0.0 collective-permute-done.3.high
  11.1 3.0 %collective-permute-done.2.low = f32[3,8,2,256]{3,2,1,0:T(2,128)S(1)} collective-permute-done((f32[3,8,2,256]{3,2,1,0:T(2,128)S(1)}, f32[3,8,2,256]{3,2,1,0:T(2,128)S(1)}, u32[]{:S(2)}, u32[]{:S(2)}) %collective-permute-start.2) | collective-permute-done | bytes 49184 | tf_op jit(solution)/shard_map/ppermute | solution.py:330
  14.1 0.1 collective-permute-start.5
  14.2 4.7 %collective-permute-start.4 = (f32[3,2,4,256]{3,2,1,0:T(4,128)S(1)}, f32[3,2,4,256]{3,2,1,0:T(4,128)S(1)}, u32[]{:S(2)}, u32[]{:S(2)}) collective-permute-start(f32[3,2,4,256]{3,2,1,0:T(4,128)S(1)} %get-tuple-element.27), channel_id=1, source_target_pairs={{0,4},{4,8},{8,12},{12,16},{16,20},{20,24},{24,28},{28,0},{1,5},{5... | collective-permute-start | bytes 73736 | tf_op jit(solution)/shard_map/ppermute | solution.py:335
  18.9 8.9 %inner.1 = (f32[2,72,256]{2,1,0:T(8,128)S(1)}, f32[6,64,256]{2,1,0:T(8,128)S(1)}, f32[6,4,72,256]{3,2,1,0:T(8,128)S(1)}, f32[6,6,72,256]{3,2,1,0:T(8,128)S(1)}, ...) custom-call(f32[3,8,64,256]{3,2,1,0:T(8,128)S(1)} %copy-done, ...), custom_call_target="tpu_custom_call" | custom-call | flops 60000000 | bytes 6000000 | tf_op jit(solution)/shard_map/inner/pallas_call | solution.py:347
  27.8 0.0 collective-permute-done.5.right_edge
  27.8 0.0 collective-permute-done.4.left_edge
  27.9 0.0 collective-permute-done.1.right
  27.9 0.0 collective-permute-done.left
  27.9 7.2 %outer.1 = (f32[2,72]{1,0:T(2,128)S(1)}, f32[2,64,256]{2,1,0:T(8,128)S(1)}) custom-call(f32[3,8,64,256]{3,2,1,0:T(8,128)S(1)} %copy-done, f32[3,2,64,256]{3,2,1,0:T(8,128)S(1)} %collective-permute-done.left, f32[3,2,64,256]{3,2,1,0:T(8,128)S(1)} %collective-permute-done.1.right, f32[3,8,2,256]{3,2,1,0:T(2,128)S(1)} %collective-permute-done.2.low, ...), custom_call_target="tpu_custom_call" | custom-call | flops 40000000 | bytes 6000000 | tf_op jit(solution)/shard_map/outer/pallas_call | solution.py:358
  35.1 0.1 collective-permute-start.6
  35.2 3.6 %collective-permute-done.6 = f32[2,72]{1,0:T(2,128)S(1)} collective-permute-done((f32[2,72]{1,0:T(2,128)S(1)}, f32[2,72]{1,0:T(2,128)S(1)}, u32[]{:S(2)}, u32[]{:S(2)}) %collective-permute-start.6) | collective-permute-done | bytes 608 | tf_op jit(solution)/shard_map/ppermute | solution.py:317
  38.8 0.0 collective-permute-start.7
  38.8 3.6 %collective-permute-done.7 = f32[2,72]{1,0:T(2,128)S(1)} collective-permute-done((f32[2,72]{1,0:T(2,128)S(1)}, f32[2,72]{1,0:T(2,128)S(1)}, u32[]{:S(2)}, u32[]{:S(2)}) %collective-permute-start.7) | collective-permute-done | bytes 608 | tf_op jit(solution)/shard_map/ppermute | solution.py:317
  42.4 0.0 collective-permute-start.8
  42.4 4.5 %collective-permute-done.8 = f32[2,72]{1,0:T(2,128)S(1)} collective-permute-done((f32[2,72]{1,0:T(2,128)S(1)}, f32[2,72]{1,0:T(2,128)S(1)}, u32[]{:S(2)}, u32[]{:S(2)}) %collective-permute-start.8) | collective-permute-done | bytes 608 | tf_op jit(solution)/shard_map/ppermute | solution.py:317
  46.8 0.9 %final.1 = (f32[1,64]{1,0:T(1,128)}, f32[8,64,256]{2,1,0:T(8,128)}) custom-call(f32[2,72]{1,0:T(2,128)S(1)} %add.11.totals, f32[6,64,256]{2,1,0:T(8,128)S(1)} %get-tuple-element.18.strength_inner, f32[2,64,256]{2,1,0:T(8,128)S(1)} %get-tuple-element.19.strength_outer), custom_call_target="tpu_custom_call" | custom-call | tf_op jit(solution)/shard_map/final/pallas_call | solution.py:371
  (5 shorter events, 0.1 us)
Async XLA Ops:
  0.6 6.1 %copy-start = (f32[3,8,64,256]{3,2,1,0:T(8,128)S(1)}, f32[3,8,64,256]{3,2,1,0:T(8,128)}, u32[]{:S(2)}) copy-start(f32[3,8,64,256]{3,2,1,0:T(8,128)} %v.3) | copy-start | bytes 4718596
  2.0 25.9 %collective-permute-start.1 = (f32[3,2,64,256]{3,2,1,0:T(8,128)S(1)}, f32[3,2,64,256]{3,2,1,0:T(8,128)S(1)}, u32[]{:S(2)}, u32[]{:S(2)}) collective-permute-start(f32[3,2,64,256]{3,2,1,0:T(8,128)S(1)} %get-tuple-element.24), channel_id=1, source_target_pairs={{0,28},{4,0},{8,4},{12,8},{16,12},{20,16},{24,20},{28,24},{1,29},{... | collective-permute-start | bytes 1179656 | tf_op jit(solution)/shard_map/ppermute | solution.py:333
  2.5 25.3 %collective-permute-start = (f32[3,2,64,256]{3,2,1,0:T(8,128)S(1)}, f32[3,2,64,256]{3,2,1,0:T(8,128)S(1)}, u32[]{:S(2)}, u32[]{:S(2)}) collective-permute-start(f32[3,2,64,256]{3,2,1,0:T(8,128)S(1)} %get-tuple-element.25), channel_id=1, source_target_pairs={{0,4},{4,8},{8,12},{12,16},{16,20},{20,24},{24,28},{28,0},{1,5},{5... | collective-permute-start | bytes 1179656 | tf_op jit(solution)/shard_map/ppermute | solution.py:332
  6.8 4.3 %collective-permute-start.3 = (f32[3,8,2,256]{3,2,1,0:T(2,128)S(1)}, f32[3,8,2,256]{3,2,1,0:T(2,128)S(1)}, u32[]{:S(2)}, u32[]{:S(2)}) collective-permute-start(f32[3,8,2,256]{3,2,1,0:T(2,128)S(1)} %get-tuple-element.22), channel_id=1, source_target_pairs={{1,0},{2,1},{3,2},{5,4},{6,5},{7,6},{9,8},{10,9},{11,10},{13,12},{... | collective-permute-start | bytes 147464 | tf_op jit(solution)/shard_map/ppermute | solution.py:331
  8.7 5.4 %collective-permute-start.2 = (f32[3,8,2,256]{3,2,1,0:T(2,128)S(1)}, f32[3,8,2,256]{3,2,1,0:T(2,128)S(1)}, u32[]{:S(2)}, u32[]{:S(2)}) collective-permute-start(f32[3,8,2,256]{3,2,1,0:T(2,128)S(1)} %get-tuple-element.23), channel_id=1, source_target_pairs={{0,1},{1,2},{2,3},{4,5},{5,6},{6,7},{8,9},{9,10},{10,11},{12,13},{... | collective-permute-start | bytes 147464 | tf_op jit(solution)/shard_map/ppermute | solution.py:330
  14.1 13.7 %collective-permute-start.5 = (f32[3,2,4,256]{3,2,1,0:T(4,128)S(1)}, f32[3,2,4,256]{3,2,1,0:T(4,128)S(1)}, u32[]{:S(2)}, u32[]{:S(2)}) collective-permute-start(f32[3,2,4,256]{3,2,1,0:T(4,128)S(1)} %get-tuple-element.26), channel_id=1, source_target_pairs={{0,28},{4,0},{8,4},{12,8},{16,12},{20,16},{24,20},{28,24},{1,29},{... | collective-permute-start | bytes 73736 | tf_op jit(solution)/shard_map/ppermute | solution.py:336
  14.2 13.6 %collective-permute-start.4 = (f32[3,2,4,256]{3,2,1,0:T(4,128)S(1)}, f32[3,2,4,256]{3,2,1,0:T(4,128)S(1)}, u32[]{:S(2)}, u32[]{:S(2)}) collective-permute-start(f32[3,2,4,256]{3,2,1,0:T(4,128)S(1)} %get-tuple-element.27), channel_id=1, source_target_pairs={{0,4},{4,8},{8,12},{12,16},{16,20},{20,24},{24,28},{28,0},{1,5},{5... | collective-permute-start | bytes 73736 | tf_op jit(solution)/shard_map/ppermute | solution.py:335
  35.1 3.6 %collective-permute-start.6 = (f32[2,72]{1,0:T(2,128)S(1)}, f32[2,72]{1,0:T(2,128)S(1)}, u32[]{:S(2)}, u32[]{:S(2)}) collective-permute-start(f32[2,72]{1,0:T(2,128)S(1)} %get-tuple-element.17), channel_id=1, source_target_pairs={{0,4},{4,0},{8,12},{12,8},{16,20},{20,16},{24,28},{28,24},{1,5},{5... | collective-permute-start | bytes 1736 | tf_op jit(solution)/shard_map/ppermute | solution.py:317
  38.8 3.6 %collective-permute-start.7 = (f32[2,72]{1,0:T(2,128)S(1)}, f32[2,72]{1,0:T(2,128)S(1)}, u32[]{:S(2)}, u32[]{:S(2)}) collective-permute-start(f32[2,72]{1,0:T(2,128)S(1)} %add.9), channel_id=1, source_target_pairs={{0,8},{4,12},{8,0},{12,4},{16,24},{20,28},{24,16},{28,20},{1,9},{5... | collective-permute-start | bytes 1736 | tf_op jit(solution)/shard_map/ppermute | solution.py:317
  42.4 4.5 %collective-permute-start.8 = (f32[2,72]{1,0:T(2,128)S(1)}, f32[2,72]{1,0:T(2,128)S(1)}, u32[]{:S(2)}, u32[]{:S(2)}) collective-permute-start(f32[2,72]{1,0:T(2,128)S(1)} %add.10), channel_id=1, source_target_pairs={{0,16},{4,20},{8,24},{12,28},{16,0},{20,4},{24,8},{28,12},{1,17},{... | collective-permute-start | bytes 1736 | tf_op jit(solution)/shard_map/ppermute | solution.py:317

commit v3 on v2

--- a/solution.py
+++ b/solution.py
@@ -327,10 +327,12 @@
 
     to_next = shift(stream_count, 1, True)
     to_last = shift(stream_count, -1, True)
+    sent_left = v[:, own - 2 :]
+    later, sent_left = lax.optimization_barrier((v, sent_left))
     low = lax.ppermute(v[:, :, rows - 2 :], "gy", shift(wall_count, 1, False))
     high = lax.ppermute(v[:, :, :2], "gy", shift(wall_count, -1, False))
-    left = lax.ppermute(v[:, own - 2 :], "gx", to_next)
-    right = lax.ppermute(v[:, :2], "gx", to_last)
+    left = lax.ppermute(sent_left, "gx", to_next)
+    right = lax.ppermute(later[:, :2], "gx", to_last)
     edges = jnp.concatenate([low, high], axis=2)
     left_edge = lax.ppermute(edges[:, own - 2 :], "gx", to_next)
     right_edge = lax.ppermute(edges[:, :2], "gx", to_last)

time: 47.9 us -> 49.9 us (1.042)
  local copies, waits for them, and re-layouts: 1.35 us -> 3.24 us
    slice x1, local copies, waits for them, and re-layouts: 0.04 us -> 1.06 us  [local(): high = lax.ppermute(v[:, :, :2], 'gy', shift(wall_count, -1, False))]
    slice x1 -> x2, local copies, waits for them, and re-layouts: 1.31 us -> 2.17 us  [the longest x1 1.14 us: local(): sent_left = v[:, own - 2:]]
  transfers between devices with their start and end apart: 9 -> 9, of which waited for: 4 -> 4; matrix products, arithmetic and copies ran while one was open for 0% -> 2% of each run, Pallas kernels for 19% -> 18%
where the time goes in v3:
time: 49.9 us; the launch traced here: 49.6 us
  Pallas kernels  17.1 us (34%)
  waiting for transfers between devices  14.6 us (29%)
  starting transfers between devices  13.9 us (28%)
  local copies, waits for them, and re-layouts  3.24 us (6%)
  between operations  0.75 us (2%)
    ppermute x3, waiting for transfers between devices, sum_over(): lax.ppermute(value, axis, [(i, i ^ step) for i in range(count)])  11.6 us
    pallas_call x1, Pallas kernels, local(): pl.pallas_call(inner_kernel, out_shape=(float_array((2, tall, span)), flo...  8.91 us
    pallas_call x1, Pallas kernels, local(): pl.pallas_call(outer_kernel, out_shape=(float_array((2, tall)), float_arr...  7.25 us
    ppermute x1, starting transfers between devices, local(): left_edge = lax.ppermute(edges[:, own - 2:], 'gx', to_next)  4.71 us
    ppermute x1, starting transfers between devices, local(): left = lax.ppermute(sent_left, 'gx', to_next)  4.19 us
    ppermute x1, waiting for transfers between devices, local(): low = lax.ppermute(v[:, :, rows - 2:], 'gy', shift(wall_count, 1, False))  2.99 us
    ppermute x1, starting transfers between devices, local(): low = lax.ppermute(v[:, :, rows - 2:], 'gy', shift(wall_count, 1, False))  2.4 us
    ppermute x1, starting transfers between devices, local(): high = lax.ppermute(v[:, :, :2], 'gy', shift(wall_count, -1, False))  1.92 us
  transfers between devices with their start and end apart: 9, of which 4 were waited for; matrix products, arithmetic and copies ran while one was open for 2% of the time, Pallas kernels for 18%

profile of v3, /device:TPU:30, one launch (start us, length us, event | category | flops | bytes accessed | tf_op | source)
XLA Modules:
  0.0 49.6 jit_solution(8950540154705503366)
XLA Ops:
  0.6 0.0 copy-start
  0.6 1.1 %slice.18 = f32[3,2,64,256]{3,2,1,0:T(8,128)S(1)} slice(f32[3,8,64,256]{3,2,1,0:T(8,128)} %v.3), slice={[0:3], [6:8], [0:64], [0:256]} | slice | bytes 786432 | tf_op jit(solution)/shard_map/slice | solution.py:330
  1.8 1.0 %slice.19 = f32[3,2,64,256]{3,2,1,0:T(8,128)S(1)} slice(f32[3,8,64,256]{3,2,1,0:T(8,128)} %v.3), slice={[0:3], [0:2], [0:64], [0:256]} | slice | bytes 786432 | tf_op jit(solution)/shard_map/slice | solution.py:335
  2.8 0.6 %collective-permute-start.1 = (f32[3,2,64,256]{3,2,1,0:T(8,128)S(1)}, f32[3,2,64,256]{3,2,1,0:T(8,128)S(1)}, u32[]{:S(2)}, u32[]{:S(2)}) collective-permute-start(f32[3,2,64,256]{3,2,1,0:T(8,128)S(1)} %slice.19), channel_id=1, source_target_pairs={{0,28},{4,0},{8,4},{12,8},{16,12},{20,16},{24,20},{28,24},{1,29},{... | collective-permute-start | bytes 1179656 | tf_op jit(solution)/shard_map/ppermute | solution.py:335
  3.4 4.2 %collective-permute-start = (f32[3,2,64,256]{3,2,1,0:T(8,128)S(1)}, f32[3,2,64,256]{3,2,1,0:T(8,128)S(1)}, u32[]{:S(2)}, u32[]{:S(2)}) collective-permute-start(f32[3,2,64,256]{3,2,1,0:T(8,128)S(1)} %slice.18), channel_id=1, source_target_pairs={{0,4},{4,8},{8,12},{12,16},{16,20},{20,24},{24,28},{28,0},{1,5},{5... | collective-permute-start | bytes 1179656 | tf_op jit(solution)/shard_map/ppermute | solution.py:334
  7.6 1.1 %fusion = (f32[3,8,2,256]{3,2,1,0:T(2,128)S(1)}, f32[3,8,2,256]{3,2,1,0:T(2,128)S(1)}) fusion(f32[3,8,64,256]{3,2,1,0:T(8,128)} %v.3), kind=kLoop, calls=%fused_computation.2 | loop fusion | bytes 196608 | tf_op jit(solution)/shard_map/slice | solution.py:333
  8.7 1.9 %collective-permute-start.3 = (f32[3,8,2,256]{3,2,1,0:T(2,128)S(1)}, f32[3,8,2,256]{3,2,1,0:T(2,128)S(1)}, u32[]{:S(2)}, u32[]{:S(2)}) collective-permute-start(f32[3,8,2,256]{3,2,1,0:T(2,128)S(1)} %get-tuple-element.26), channel_id=1, source_target_pairs={{1,0},{2,1},{3,2},{5,4},{6,5},{7,6},{9,8},{10,9},{11,10},{13,12},{... | collective-permute-start | bytes 147464 | tf_op jit(solution)/shard_map/ppermute | solution.py:333
  10.6 2.4 %collective-permute-start.2 = (f32[3,8,2,256]{3,2,1,0:T(2,128)S(1)}, f32[3,8,2,256]{3,2,1,0:T(2,128)S(1)}, u32[]{:S(2)}, u32[]{:S(2)}) collective-permute-start(f32[3,8,2,256]{3,2,1,0:T(2,128)S(1)} %get-tuple-element.27), channel_id=1, source_target_pairs={{0,1},{1,2},{2,3},{4,5},{5,6},{6,7},{8,9},{9,10},{10,11},{12,13},{... | collective-permute-start | bytes 147464 | tf_op jit(solution)/shard_map/ppermute | solution.py:332
  13.0 0.0 collective-permute-done.3.high
  13.0 3.0 %collective-permute-done.2.low = f32[3,8,2,256]{3,2,1,0:T(2,128)S(1)} collective-permute-done((f32[3,8,2,256]{3,2,1,0:T(2,128)S(1)}, f32[3,8,2,256]{3,2,1,0:T(2,128)S(1)}, u32[]{:S(2)}, u32[]{:S(2)}) %collective-permute-start.2) | collective-permute-done | bytes 49184 | tf_op jit(solution)/shard_map/ppermute | solution.py:332
  16.0 0.1 collective-permute-start.5
  16.1 4.7 %collective-permute-start.4 = (f32[3,2,4,256]{3,2,1,0:T(4,128)S(1)}, f32[3,2,4,256]{3,2,1,0:T(4,128)S(1)}, u32[]{:S(2)}, u32[]{:S(2)}) collective-permute-start(f32[3,2,4,256]{3,2,1,0:T(4,128)S(1)} %get-tuple-element.29), channel_id=1, source_target_pairs={{0,4},{4,8},{8,12},{12,16},{16,20},{20,24},{24,28},{28,0},{1,5},{5... | collective-permute-start | bytes 73736 | tf_op jit(solution)/shard_map/ppermute | solution.py:337
  20.8 0.0 copy-done
  20.8 8.9 %inner.1 = (f32[2,72,256]{2,1,0:T(8,128)S(1)}, f32[6,64,256]{2,1,0:T(8,128)S(1)}, f32[6,4,72,256]{3,2,1,0:T(8,128)S(1)}, f32[6,6,72,256]{3,2,1,0:T(8,128)S(1)}, ...) custom-call(f32[3,8,64,256]{3,2,1,0:T(8,128)S(1)} %copy-done, ...), custom_call_target="tpu_custom_call" | custom-call | flops 60000000 | bytes 6000000 | tf_op jit(solution)/shard_map/inner/pallas_call | solution.py:349
  29.7 0.0 collective-permute-done.5.right_edge
  29.7 0.0 collective-permute-done.4.left_edge
  29.7 0.0 collective-permute-done.1.right
  29.8 0.0 collective-permute-done.left
  29.8 7.2 %outer.1 = (f32[2,72]{1,0:T(2,128)S(1)}, f32[2,64,256]{2,1,0:T(8,128)S(1)}) custom-call(f32[3,8,64,256]{3,2,1,0:T(8,128)S(1)} %copy-done, f32[3,2,64,256]{3,2,1,0:T(8,128)S(1)} %collective-permute-done.left, f32[3,2,64,256]{3,2,1,0:T(8,128)S(1)} %collective-permute-done.1.right, f32[3,8,2,256]{3,2,1,0:T(2,128)S(1)} %collective-permute-done.2.low, ...), custom_call_target="tpu_custom_call" | custom-call | flops 40000000 | bytes 6000000 | tf_op jit(solution)/shard_map/outer/pallas_call | solution.py:360
  37.0 0.1 collective-permute-start.6
  37.1 3.6 %collective-permute-done.6 = f32[2,72]{1,0:T(2,128)S(1)} collective-permute-done((f32[2,72]{1,0:T(2,128)S(1)}, f32[2,72]{1,0:T(2,128)S(1)}, u32[]{:S(2)}, u32[]{:S(2)}) %collective-permute-start.6) | collective-permute-done | bytes 608 | tf_op jit(solution)/shard_map/ppermute | solution.py:317
  40.7 0.0 collective-permute-start.7
  40.7 3.6 %collective-permute-done.7 = f32[2,72]{1,0:T(2,128)S(1)} collective-permute-done((f32[2,72]{1,0:T(2,128)S(1)}, f32[2,72]{1,0:T(2,128)S(1)}, u32[]{:S(2)}, u32[]{:S(2)}) %collective-permute-start.7) | collective-permute-done | bytes 608 | tf_op jit(solution)/shard_map/ppermute | solution.py:317
  44.2 0.0 collective-permute-start.8
  44.3 4.5 %collective-permute-done.8 = f32[2,72]{1,0:T(2,128)S(1)} collective-permute-done((f32[2,72]{1,0:T(2,128)S(1)}, f32[2,72]{1,0:T(2,128)S(1)}, u32[]{:S(2)}, u32[]{:S(2)}) %collective-permute-start.8) | collective-permute-done | bytes 608 | tf_op jit(solution)/shard_map/ppermute | solution.py:317
  48.7 0.9 %final.1 = (f32[1,64]{1,0:T(1,128)}, f32[8,64,256]{2,1,0:T(8,128)}) custom-call(f32[2,72]{1,0:T(2,128)S(1)} %add.11.totals, f32[6,64,256]{2,1,0:T(8,128)S(1)} %get-tuple-element.22.strength_inner, f32[2,64,256]{2,1,0:T(8,128)S(1)} %get-tuple-element.23.strength_outer), custom_call_target="tpu_custom_call" | custom-call | tf_op jit(solution)/shard_map/final/pallas_call | solution.py:373
  (4 shorter events, 0.0 us)
Async XLA Ops:
  0.6 20.2 %copy-start = (f32[3,8,64,256]{3,2,1,0:T(8,128)S(1)}, f32[3,8,64,256]{3,2,1,0:T(8,128)}, u32[]{:S(2)}) copy-start(f32[3,8,64,256]{3,2,1,0:T(8,128)} %v.3) | copy-start | bytes 4718596
  2.8 26.9 %collective-permute-start.1 = (f32[3,2,64,256]{3,2,1,0:T(8,128)S(1)}, f32[3,2,64,256]{3,2,1,0:T(8,128)S(1)}, u32[]{:S(2)}, u32[]{:S(2)}) collective-permute-start(f32[3,2,64,256]{3,2,1,0:T(8,128)S(1)} %slice.19), channel_id=1, source_target_pairs={{0,28},{4,0},{8,4},{12,8},{16,12},{20,16},{24,20},{28,24},{1,29},{... | collective-permute-start | bytes 1179656 | tf_op jit(solution)/shard_map/ppermute | solution.py:335
  3.4 26.3 %collective-permute-start = (f32[3,2,64,256]{3,2,1,0:T(8,128)S(1)}, f32[3,2,64,256]{3,2,1,0:T(8,128)S(1)}, u32[]{:S(2)}, u32[]{:S(2)}) collective-permute-start(f32[3,2,64,256]{3,2,1,0:T(8,128)S(1)} %slice.18), channel_id=1, source_target_pairs={{0,4},{4,8},{8,12},{12,16},{16,20},{20,24},{24,28},{28,0},{1,5},{5... | collective-permute-start | bytes 1179656 | tf_op jit(solution)/shard_map/ppermute | solution.py:334
  8.7 4.3 %collective-permute-start.3 = (f32[3,8,2,256]{3,2,1,0:T(2,128)S(1)}, f32[3,8,2,256]{3,2,1,0:T(2,128)S(1)}, u32[]{:S(2)}, u32[]{:S(2)}) collective-permute-start(f32[3,8,2,256]{3,2,1,0:T(2,128)S(1)} %get-tuple-element.26), channel_id=1, source_target_pairs={{1,0},{2,1},{3,2},{5,4},{6,5},{7,6},{9,8},{10,9},{11,10},{13,12},{... | collective-permute-start | bytes 147464 | tf_op jit(solution)/shard_map/ppermute | solution.py:333
  10.6 5.4 %collective-permute-start.2 = (f32[3,8,2,256]{3,2,1,0:T(2,128)S(1)}, f32[3,8,2,256]{3,2,1,0:T(2,128)S(1)}, u32[]{:S(2)}, u32[]{:S(2)}) collective-permute-start(f32[3,8,2,256]{3,2,1,0:T(2,128)S(1)} %get-tuple-element.27), channel_id=1, source_target_pairs={{0,1},{1,2},{2,3},{4,5},{5,6},{6,7},{8,9},{9,10},{10,11},{12,13},{... | collective-permute-start | bytes 147464 | tf_op jit(solution)/shard_map/ppermute | solution.py:332
  16.0 13.7 %collective-permute-start.5 = (f32[3,2,4,256]{3,2,1,0:T(4,128)S(1)}, f32[3,2,4,256]{3,2,1,0:T(4,128)S(1)}, u32[]{:S(2)}, u32[]{:S(2)}) collective-permute-start(f32[3,2,4,256]{3,2,1,0:T(4,128)S(1)} %get-tuple-element.28), channel_id=1, source_target_pairs={{0,28},{4,0},{8,4},{12,8},{16,12},{20,16},{24,20},{28,24},{1,29},{... | collective-permute-start | bytes 73736 | tf_op jit(solution)/shard_map/ppermute | solution.py:338
  16.1 13.6 %collective-permute-start.4 = (f32[3,2,4,256]{3,2,1,0:T(4,128)S(1)}, f32[3,2,4,256]{3,2,1,0:T(4,128)S(1)}, u32[]{:S(2)}, u32[]{:S(2)}) collective-permute-start(f32[3,2,4,256]{3,2,1,0:T(4,128)S(1)} %get-tuple-element.29), channel_id=1, source_target_pairs={{0,4},{4,8},{8,12},{12,16},{16,20},{20,24},{24,28},{28,0},{1,5},{5... | collective-permute-start | bytes 73736 | tf_op jit(solution)/shard_map/ppermute | solution.py:337
  37.0 3.6 %collective-permute-start.6 = (f32[2,72]{1,0:T(2,128)S(1)}, f32[2,72]{1,0:T(2,128)S(1)}, u32[]{:S(2)}, u32[]{:S(2)}) collective-permute-start(f32[2,72]{1,0:T(2,128)S(1)} %get-tuple-element.21), channel_id=1, source_target_pairs={{0,4},{4,0},{8,12},{12,8},{16,20},{20,16},{24,28},{28,24},{1,5},{5... | collective-permute-start | bytes 1736 | tf_op jit(solution)/shard_map/ppermute | solution.py:317
  40.7 3.6 %collective-permute-start.7 = (f32[2,72]{1,0:T(2,128)S(1)}, f32[2,72]{1,0:T(2,128)S(1)}, u32[]{:S(2)}, u32[]{:S(2)}) collective-permute-start(f32[2,72]{1,0:T(2,128)S(1)} %add.9), channel_id=1, source_target_pairs={{0,8},{4,12},{8,0},{12,4},{16,24},{20,28},{24,16},{28,20},{1,9},{5... | collective-permute-start | bytes 1736 | tf_op jit(solution)/shard_map/ppermute | solution.py:317
  44.2 4.5 %collective-permute-start.8 = (f32[2,72]{1,0:T(2,128)S(1)}, f32[2,72]{1,0:T(2,128)S(1)}, u32[]{:S(2)}, u32[]{:S(2)}) collective-permute-start(f32[2,72]{1,0:T(2,128)S(1)} %add.10), channel_id=1, source_target_pairs={{0,16},{4,20},{8,24},{12,28},{16,0},{20,4},{24,8},{28,12},{1,17},{... | collective-permute-start | bytes 1736 | tf_op jit(solution)/shard_map/ppermute | solution.py:317
